TPU v7x, 32 devices: a whole 2x2x4 slice. The times are simulated.
32 devices in a mesh: seg: 32 (over z, y, x, core).
Axes of the slice: x: 2, y: 2, z: 4, core: 2. Of those that a mesh axis runs over, the one named last changes fastest.
Arguments:
- tokens: bfloat16 [8192, 3584], P('seg'), may hold values from -6 to 6
- memory: bfloat16 [64, 3584], replicated, may hold values from -6 to 6
- norm_gain: float32 [3584], replicated, may hold values from 0.5 to 2
- post_gain: float32 [3584], replicated, may hold values from 0.5 to 2
- query_weight: bfloat16 [3584, 2048], P('seg'), may hold values from -0.09375 to 0.09375
- key_matrix: bfloat16 [3584, 1024], replicated, may hold values from -0.09375 to 0.09375
- value_matrix: bfloat16 [3584, 1024], replicated, may hold values from -0.09375 to 0.09375
- output_weight: bfloat16 [2048, 3584], P('seg'), may hold values from -0.125 to 0.125
- segment_weight: float32 [32], P('seg'), may hold values from 0.1 to 4
Outputs:
- token_out: bfloat16 [8192, 3584], P('seg')
- memory_out: bfloat16 [2048, 3584], P('seg')
- changes: float32 [3], replicated
All inputs are finite; a program needn't handle non-finite values.
Results may differ from a plain program's by a relative error of at most 0.014.
Values may be sent and summed in bfloat16 or wider, within the bound.
A program may use at most 192 MiB of HBM per device.

v0:
```python
import functools

import jax
import jax.numpy as jnp
from jax import lax
from jax.experimental import pallas as pl
from jax.experimental.pallas import tpu as pltpu
from jax.sharding import PartitionSpec as P


HEAD_WIDTH = 256
KEY_VALUE_HEADS = 4
ITERS = 3
LANES = 128
MESH = pl.DeviceIdType.MESH


eps = 1e-06


def from_behind(block, axis, distance):
    devices = range(lax.axis_size(axis))
    route = [(i - distance, i) for i in devices if i - distance in devices]
    return lax.ppermute(block, axis, route)


def prenorm(rows, gain):
    rows = rows.astype(jnp.float32)
    mean_sq = jnp.mean(rows * rows, axis=-1, keepdims=True)
    return (rows / jnp.sqrt(mean_sq + eps) * gain).astype(jnp.bfloat16)


def reduce_kernel(n, scale, part_ref, out_ref, held, total, final, send1, recv1, send2, recv2):
    me = lax.axis_index("seg") // 2
    core = lax.rem(lax.axis_index("seg"), 2)

    def scatter(k):
        to = lax.rem(me + k, n)
        return pltpu.make_async_remote_copy(
            src_ref=part_ref.at[to],
            dst_ref=held.at[k],
            send_sem=send1.at[k],
            recv_sem=recv1.at[k],
            device_id=(2 * to + core,),
            device_id_type=MESH,
        )

    def spread(k):
        to = lax.rem(me + k, n)
        return pltpu.make_async_remote_copy(
            src_ref=final,
            dst_ref=out_ref.at[me],
            send_sem=send2.at[k],
            recv_sem=recv2.at[k],
            device_id=(2 * to + core,),
            device_id_type=MESH,
        )

    @pl.loop(1, n)
    def _(k):
        scatter(k).start()

    total[...] = part_ref[me]

    @pl.loop(1, n)
    def _(k):
        scatter(k).wait_recv()
        total[...] += held[k]

    final[...] = (total[...] * scale).astype(final.dtype)

    @pl.loop(1, n)
    def _(k):
        spread(k).start()

    out_ref[me] = final[...]

    @pl.loop(1, n)
    def _(k):
        scatter(k).wait_send()
        spread(k).wait()


def all_sum(parts, scale):
    n = parts.shape[0]
    sems = pltpu.SemaphoreType.DMA((n,))
    return pl.pallas_call(
        functools.partial(reduce_kernel, n, scale),
        out_shape=jax.ShapeDtypeStruct(parts.shape, jnp.bfloat16),
        in_specs=[pl.BlockSpec(memory_space=pltpu.VMEM)],
        out_specs=pl.BlockSpec(memory_space=pltpu.VMEM),
        scratch_shapes=[
            pltpu.VMEM(parts.shape, parts.dtype),
            pltpu.VMEM(parts.shape[1:], parts.dtype),
            pltpu.VMEM(parts.shape[1:], jnp.bfloat16),
            sems,
            sems,
            sems,
            sems,
        ],
        compiler_params=pltpu.CompilerParams(has_side_effects=True),
        cost_estimate=pl.CostEstimate(flops=0, bytes_accessed=30_000_000, transcendentals=0),
        name="query_sum",
    )(parts)


def total_kernel(n, part_ref, out_ref, held, send, recv):
    me = lax.axis_index("seg")

    def copy(k):
        return pltpu.make_async_remote_copy(
            src_ref=part_ref,
            dst_ref=held.at[me],
            send_sem=send.at[k],
            recv_sem=recv.at[k],
            device_id=(lax.rem(me + k, n),),
            device_id_type=MESH,
        )

    @pl.loop(1, n)
    def _(k):
        copy(k).start()

    held[me] = part_ref[...]

    @pl.loop(1, n)
    def _(k):
        copy(k).wait()

    out_ref[...] = jnp.sum(held[...], axis=0)


def small_sum(part, n):
    sems = pltpu.SemaphoreType.DMA((n,))
    return pl.pallas_call(
        functools.partial(total_kernel, n),
        out_shape=jax.ShapeDtypeStruct(part.shape, part.dtype),
        in_specs=[pl.BlockSpec(memory_space=pltpu.VMEM)],
        out_specs=pl.BlockSpec(memory_space=pltpu.VMEM),
        scratch_shapes=[pltpu.VMEM((n,) + part.shape, part.dtype), sems, sems],
        compiler_params=pltpu.CompilerParams(has_side_effects=True),
        cost_estimate=pl.CostEstimate(flops=0, bytes_accessed=8_000_000, transcendentals=0),
        name="change_sum",
    )(part)


def attend_kernel(first, keys, q_ref, rk_ref, rv_ref, k_ref, v_ref, out_ref):
    rows = q_ref.shape[0]
    nt = (((1,), (1,)), ((), ()))
    row = lax.broadcasted_iota(jnp.int32, (rows, keys), 0)
    col = lax.broadcasted_iota(jnp.int32, (rows, keys), 1)
    allowed = col <= row + first
    for half in range(2):
        cols = slice(half * HEAD_WIDTH, (half + 1) * HEAD_WIDTH)
        q = q_ref[:, cols]
        own = lax.dot_general(q, k_ref[:keys], nt, preferred_element_type=jnp.float32)
        own = jnp.where(allowed, jnp.exp(own), 0.0)
        read = jnp.exp(
            lax.dot_general(q, rk_ref[...], nt, preferred_element_type=jnp.float32)
        )
        denom = jnp.sum(own, axis=-1, keepdims=True) + jnp.sum(read, axis=-1, keepdims=True)
        numer = jnp.dot(
            own.astype(jnp.bfloat16), v_ref[:keys], preferred_element_type=jnp.float32
        ) + jnp.dot(read.astype(jnp.bfloat16), rv_ref[...], preferred_element_type=jnp.float32)
        out_ref[:, cols] = (numer / denom).astype(jnp.bfloat16)


def attend(q, read_k, read_v, local_k, local_v, first, keys):
    rows, width = q.shape
    mem, total = read_k.shape[0], local_k.shape[0]
    at = lambda h: (0, h)
    return pl.pallas_call(
        functools.partial(attend_kernel, first, keys),
        grid=(KEY_VALUE_HEADS,),
        out_shape=jax.ShapeDtypeStruct((rows, width), jnp.bfloat16),
        in_specs=[
            pl.BlockSpec((rows, 2 * HEAD_WIDTH), at),
            pl.BlockSpec((mem, HEAD_WIDTH), at),
            pl.BlockSpec((mem, HEAD_WIDTH), at),
            pl.BlockSpec((total, HEAD_WIDTH), at),
            pl.BlockSpec((total, HEAD_WIDTH), at),
        ],
        out_specs=pl.BlockSpec((rows, 2 * HEAD_WIDTH), at),
        cost_estimate=pl.CostEstimate(
            flops=4 * rows * width * (keys + mem), bytes_accessed=6_000_000, transcendentals=0
        ),
        name="attend",
    )(q, read_k, read_v, local_k, local_v)


def finish(inputs, attn, output_weight, post_gain):
    proj = jnp.dot(attn, output_weight, preferred_element_type=jnp.float32)
    mean_sq = jnp.mean(proj * proj, axis=-1, keepdims=True)
    return (inputs.astype(jnp.float32) + proj / jnp.sqrt(mean_sq + eps) * post_gain).astype(
        jnp.bfloat16
    )


def shards(
    tokens,
    memory,
    norm_gain,
    post_gain,
    query_weight,
    key_matrix,
    value_matrix,
    output_weight,
    segment_weight,
):
    n = lax.axis_size("seg")
    me = lax.axis_index("seg")
    tok_rows = tokens.shape[0]
    mem_rows, feature_width = memory.shape
    own_rows, query_width = query_weight.shape
    scale = 1.0 / HEAD_WIDTH**0.5
    output_full = lax.all_gather(output_weight, "seg", axis=0, tiled=True)

    mem_norm = prenorm(memory, norm_gain)
    own_cols = lax.dynamic_slice_in_dim(mem_norm, me * own_rows, own_rows, axis=1)
    part = jnp.dot(own_cols, query_weight, preferred_element_type=jnp.float32)
    blocks = query_width // LANES
    part = jnp.transpose(part.reshape(mem_rows, blocks, LANES), (1, 0, 2))
    core = lax.rem(me, 2)
    pairs = [(i, i + 1 - 2 * (i % 2)) for i in range(n)]
    share = blocks // 2
    kept = lax.dynamic_slice_in_dim(part, core * share, share, axis=0)
    given = lax.dynamic_slice_in_dim(part, (1 - core) * share, share, axis=0)
    kept = kept + lax.ppermute(given, "seg", pairs)
    peers = n // 2
    own_q = all_sum(kept.reshape(peers, mem_rows * share // peers, LANES), scale)
    own_q = own_q.reshape(share, mem_rows, LANES)
    other_q = lax.ppermute(own_q, "seg", pairs)
    low = core == 0
    write_q = jnp.concatenate(
        [jnp.where(low, own_q, other_q), jnp.where(low, other_q, own_q)], axis=0
    )
    write_q = jnp.transpose(write_q, (1, 0, 2)).reshape(mem_rows, query_width)

    own_query, write_q = lax.optimization_barrier((query_weight, write_q))
    query_full = lax.all_gather(own_query, "seg", axis=0, tiled=True)

    normed = prenorm(jnp.concatenate([tokens, memory], axis=0), norm_gain)
    local_k = jnp.dot(normed, key_matrix, preferred_element_type=jnp.float32).astype(jnp.bfloat16)
    local_v = jnp.dot(normed, value_matrix, preferred_element_type=jnp.float32).astype(jnp.bfloat16)
    total_rows = tok_rows + mem_rows
    first = jnp.int32(0) == me
    previous = memory
    squares = []
    own_weight = segment_weight[0]
    count_all = n * mem_rows * feature_width
    read_k, read_v = local_k[tok_rows:], local_v[tok_rows:]
    for step in range(ITERS):
        attn = attend(write_q, read_k, read_v, local_k, local_v, tok_rows, total_rows)
        newest = finish(memory, attn, output_full, post_gain)
        diff = newest.astype(jnp.float32) - previous.astype(jnp.float32)
        squares.append(jnp.sum(diff * diff) * own_weight)
        previous = newest
        if step + 1 < ITERS:
            read = jnp.where(first, memory, from_behind(newest, "seg", 1))
            read_norm = prenorm(read, norm_gain)
            read_k = jnp.dot(read_norm, key_matrix, preferred_element_type=jnp.float32).astype(
                jnp.bfloat16
            )
            read_v = jnp.dot(read_norm, value_matrix, preferred_element_type=jnp.float32).astype(
                jnp.bfloat16
            )
    squares = jnp.broadcast_to(jnp.pad(jnp.stack(squares), (0, LANES - ITERS))[None], (8, LANES))
    totals = small_sum(squares, n)[0, :ITERS]
    change_vec = jnp.sqrt(totals / count_all + eps)

    query_acc = jnp.dot(normed[:tok_rows], query_full, preferred_element_type=jnp.float32)
    query_vectors = (query_acc * scale).astype(jnp.bfloat16)
    attn = attend(query_vectors, read_k, read_v, local_k, local_v, 0, tok_rows)
    token_out = finish(tokens, attn, output_full, post_gain)
    return (token_out, previous, change_vec)


def chip_grid(chips):
    side = 1
    while (2 * side) ** 3 <= chips and chips % (4 * side * side) == 0:
        side *= 2
    return chips // (side * side), side


def fits(tokens, memory, norm_gain, post_gain, query_weight, *rest):
    n = lax.axis_size("seg")
    own_rows, query_width = query_weight.shape
    out_rows = rest[2].shape[0]
    mem_rows = memory.shape[0]
    if n % 2 or n < 8:
        return False
    _, side = chip_grid(n // 2)
    plane = 2 * side * side
    piece = mem_rows * (query_width // LANES) // n
    return (
        side == 2
        and own_rows % 16 == 0
        and out_rows % 16 == 0
        and (own_rows * plane) % LANES == 0
        and piece % 16 == 0
        and mem_rows % piece == 0
        and memory.shape[1] >= 256
        and own_rows + LANES <= 256
    )


def nearest(position, k, size):
    value = 0
    for p in range(size):
        order = sorted(range(size), key=lambda q: (abs(q - p), q))
        value = jnp.where(position == p, order[k], value)
    return value


def arrival_order(depth, side):
    sheet = sorted(
        [(k, j) for k in range(depth) for j in range(side)],
        key=lambda e: (e[0] + e[1], e[1] == 0, e[0]),
    )
    items, clock = [], 0
    for k, j in sheet:
        if k + j:
            items.append((k + j, 0, (k, j, 0)))
        clock = max(clock, k + j) + 1
        for i in range(1, side):
            items.append((clock + i - 1, 1, (k, j, i)))
    return [e for _, _, e in sorted(items)]


def fused_kernel(
    n,
    tokens_hbm,
    memory_hbm,
    norm_gain,
    post_gain,
    wq_hbm,
    wk_hbm,
    wv_hbm,
    wo_hbm,
    seg_weight,
    token_out,
    memory_out,
    change_out,
    tokens,
    memory,
    wk,
    wv,
    wq,
    wo,
    window,
    normed,
    part,
    swapped,
    kept,
    held,
    piece_out,
    pieces,
    write_q,
    local_k,
    local_v,
    sent_kv,
    read_kv,
    attn,
    proj,
    previous,
    newnorm,
    query,
    change,
    changes,
    load_sem,
    gather_send,
    gather_recv,
    pair_recv,
    swap_sem,
    sum_send,
    sum_recv,
    spread_send,
    spread_recv,
    kv_send,
    kv_recv,
    change_send,
    change_recv,
    store_sem,
):
    me = lax.axis_index("seg")
    core = lax.rem(me, 2)
    partner = me + 1 - 2 * core
    chip = me // 2
    chips = n // 2
    depth, side = chip_grid(chips)
    tok_rows, width = tokens.shape
    mem_rows = memory.shape[0]
    all_rows = tok_rows + mem_rows
    fast, mid, slow = (
        lax.rem(chip, side),
        lax.rem(chip // side, side),
        chip // (side * side),
    )
    scale = 1.0 / HEAD_WIDTH**0.5
    f32, bf16 = jnp.float32, jnp.bfloat16
    u = mid * (1 - core) + fast * core
    v = fast * (1 - core) + mid * core
    u_step = side * (1 - core) + core
    v_step = (1 - core) + side * core
    z_step = side * side
    full = (wo, wq)
    block_rows = (wo_hbm.shape[0], wq_hbm.shape[0])
    query_width = wq.shape[1]

    def hint(x, m):
        return pl.multiple_of(x, m)

    def block_at(w, device):
        rows = block_rows[w]
        return full[w].at[pl.ds(hint(device * rows, 16), rows)]

    def remote(src, dst, send, recv, device):
        return pltpu.make_async_remote_copy(
            src_ref=src,
            dst_ref=dst,
            send_sem=send,
            recv_sem=recv,
            device_id=(device,),
            device_id_type=MESH,
        )

    def place(k, j, i):
        z = nearest(slow, k, depth)
        uu = u if j == 0 else 1 - u
        vv = v if i == 0 else 1 - v
        return z, z * z_step + uu * u_step + vv * v_step

    def rank(k, j, i):
        return (k * side + j) * side + i

    def moves(w, k, j, i):
        z, origin = place(k, j, i)
        block = block_at(w, 2 * origin + core)
        ports = 5

        def copy(port, device, recv):
            return remote(
                block,
                block,
                gather_send.at[w, rank(k, j, i) * ports + port],
                recv.at[w, origin],
                device,
            )

        found = []
        if j == 0 and i == 0:
            up = slow + 1 < depth
            down = slow > 0
            if k:
                up = jnp.logical_and(up, z < slow)
                down = jnp.logical_and(down, z > slow)
            found.append((up, copy(0, me + 2 * z_step, gather_recv)))
            found.append((down, copy(1, me - 2 * z_step, gather_recv)))
        if i == 0 and j == 0:
            found.append((None, copy(2, me + 2 * u_step * (1 - 2 * u), gather_recv)))
        if i == 0:
            found.append((None, copy(3, me + 2 * v_step * (1 - 2 * v), gather_recv)))
        found.append((None, copy(4, partner, pair_recv)))
        return found

    def start(items):
        for guard, copy in items:
            if guard is None:
                copy.start()
            else:
                pl.when(guard)(copy.start)

    def arrive(w, k, j, i):
        _, origin = place(k, j, i)
        block = block_at(w, 2 * origin + core)
        remote(
            block, block, gather_send.at[w, 0], gather_recv.at[w, origin], partner
        ).wait_recv()

    def arrived(w, e):
        arrive(w, *e)
        start(moves(w, *e))

    def pair_arrive(w, k, j, i):
        _, origin = place(k, j, i)
        block = block_at(w, 2 * origin + 1 - core)
        remote(
            block, block, gather_send.at[w, 0], pair_recv.at[w, origin], partner
        ).wait_recv()

    events = arrival_order(depth, side)
    everything = [(0, 0, 0)] + events

    def load(src, dst, i):
        return pltpu.make_async_copy(src, dst, load_sem.at[i])

    off = me * block_rows[1]
    first_lane = jnp.minimum(off // LANES * LANES, width - 256)
    shift = off - first_lane
    loads = [
        load(wo_hbm, block_at(0, me), 0),
        load(memory_hbm, memory, 1),
        load(wq_hbm, block_at(1, me), 2),
        load(tokens_hbm, tokens, 3),
        load(wk_hbm, wk, 4),
        load(wv_hbm, wv, 5),
    ]
    for copy in loads:
        copy.start()
    window[...] = jnp.zeros_like(window)
    own_window = load(
        wq_hbm, window.at[pl.ds(hint(shift, 16), block_rows[1])], 6
    )
    own_window.start()

    def norm_rows(src, dst, at, rows):
        step_rows = 16

        @pl.loop(0, rows // step_rows)
        def _(t):
            here = pl.ds(hint(t * step_rows, step_rows), step_rows)
            x = src[here, :].astype(f32)
            mean_sq = jnp.sum(x * x, axis=-1, keepdims=True) / width
            there = pl.ds(hint(at + t * step_rows, step_rows), step_rows)
            dst[there, :] = (x / jnp.sqrt(mean_sq + eps) * norm_gain[...]).astype(bf16)

    def times(lhs, weight, dst, tile):
        @pl.loop(0, weight.shape[1] // tile)
        def _(t):
            cols = pl.ds(hint(t * tile, tile), tile)
            dst[:, cols] = jnp.dot(
                lhs[...], weight[:, cols], preferred_element_type=f32
            ).astype(dst.dtype)

    nt = (((1,), (1,)), ((), ()))

    def attend_rows(q_ref, rows, rk, rv, first, keys, pre):
        row = lax.broadcasted_iota(jnp.int32, (rows, keys), 0)
        col = lax.broadcasted_iota(jnp.int32, (rows, keys), 1)
        allowed = col <= row + first

        @pl.loop(0, KEY_VALUE_HEADS)
        def _(g):
            kv_cols = pl.ds(hint(g * HEAD_WIDTH, HEAD_WIDTH), HEAD_WIDTH)
            kk = local_k[0:keys, kv_cols]
            vv = local_v[0:keys, kv_cols]
            rkk = rk[:, kv_cols]
            rvv = rv[:, kv_cols]
            for half in range(2):
                cols = pl.ds(hint((2 * g + half) * HEAD_WIDTH, HEAD_WIDTH), HEAD_WIDTH)
                q = q_ref[0:rows, cols]
                if pre:
                    q = (q * scale).astype(bf16)
                own = lax.dot_general(q, kk, nt, preferred_element_type=f32)
                own = jnp.where(allowed, jnp.exp(own), 0.0)
                read = jnp.exp(lax.dot_general(q, rkk, nt, preferred_element_type=f32))
                denom = jnp.sum(own, axis=-1, keepdims=True) + jnp.sum(
                    read, axis=-1, keepdims=True
                )
                numer = jnp.dot(
                    own.astype(bf16), vv, preferred_element_type=f32
                ) + jnp.dot(read.astype(bf16), rvv, preferred_element_type=f32)
                attn[0:rows, cols] = (numer / denom).astype(bf16)

    def project(rows):
        tile = 512

        @pl.loop(0, width // tile)
        def _(t):
            cols = pl.ds(hint(t * tile, tile), tile)
            proj[0:rows, cols] = jnp.dot(
                attn[0:rows, :], wo[:, cols], preferred_element_type=f32
            )

    def layer_rows(src, here):
        p = proj[here, :]
        mean_sq = jnp.sum(p * p, axis=-1, keepdims=True) / width
        x = src[here, :].astype(f32)
        return (x + p / jnp.sqrt(mean_sq + eps) * post_gain[...]).astype(bf16)

    def write_rows(step):
        before = memory if step == 0 else previous
        change[...] = jnp.zeros_like(change) if step == 0 else change[...]
        lane = lax.broadcasted_iota(jnp.int32, change.shape, 1)

        @pl.loop(0, mem_rows // 16)
        def _(t):
            here = pl.ds(hint(t * 16, 16), 16)
            out = layer_rows(memory, here)
            o = out.astype(f32)
            diff = o - before[here, :].astype(f32)
            total = jnp.sum(diff * diff, keepdims=True)
            change[...] += jnp.where(lane == step, total * seg_weight[0], 0.0)
            previous[here, :] = out
            if step + 1 < ITERS:
                mean_sq = jnp.sum(o * o, axis=-1, keepdims=True) / width
                newnorm[here, :] = (o / jnp.sqrt(mean_sq + eps) * norm_gain[...]).astype(bf16)

    right = lax.rem(me + 1, n)

    def kv_copy(step, which):
        return remote(
            sent_kv.at[step, which],
            read_kv.at[step, which],
            kv_send.at[step, which],
            kv_recv.at[step, which],
            right,
        )

    def send_kv(step):
        for which, weight in enumerate((wk, wv)):
            times(newnorm, weight, sent_kv.at[step, which], 512)
            pl.when(me + 1 < n)(kv_copy(step, which).start)

    def wait_kv(step):
        @pl.when(me > 0)
        def _():
            for which in range(2):
                kv_copy(step, which).wait_recv()

        @pl.when(me == 0)
        def _():
            for which, local in enumerate((local_k, local_v)):
                read_kv[step, which] = local[tok_rows:all_rows, :]

    loads[0].wait()
    start(moves(0, 0, 0, 0))
    loads[1].wait()
    norm_rows(memory, normed, tok_rows, mem_rows)
    own_window.wait()
    piece = pieces.shape[1]
    per_block = mem_rows // piece
    half_width = query_width // 2
    own_cols = normed[tok_rows:all_rows, pl.ds(hint(first_lane, LANES), 256)]
    for c in range(2):
        rows_of = jnp.dot(
            own_cols,
            window[:, c * half_width : (c + 1) * half_width],
            preferred_element_type=f32,
        )
        for t in range(chips):
            at = t // per_block * LANES
            down = t % per_block * piece
            part[c, t] = rows_of[down : down + piece, at : at + LANES]
    swap = remote(part.at[1 - core], swapped, swap_sem.at[0], swap_sem.at[1], partner)
    swap.start()
    loads[3].wait()
    norm_rows(tokens, normed, 0, tok_rows)
    swap.wait_recv()
    kept[...] = part[core] + swapped[...]

    def scatter(k):
        to = lax.rem(chip + k, chips)
        return remote(
            kept.at[to], held.at[k], sum_send.at[k], sum_recv.at[k], 2 * to + core
        )

    @pl.loop(1, chips)
    def _(k):
        scatter(k).start()

    loads[4].wait()
    times(normed, wk, local_k, 512)
    early = [e for e in events if sum(e) == 1]
    late = [e for e in events if sum(e) > 1]
    for e in early:
        arrived(0, e)

    @pl.loop(1, chips)
    def _(k):
        scatter(k).wait_recv()

    piece_sum = kept[chip]
    for k in range(1, chips):
        piece_sum += held[k]
    piece_out[...] = (piece_sum * scale).astype(bf16)

    def spread(k):
        to = lax.rem(me + k, n)
        return remote(
            piece_out, pieces.at[me], spread_send.at[k], spread_recv.at[k], to
        )

    @pl.loop(1, n)
    def _(k):
        spread(k).start()

    pieces[me] = piece_out[...]
    loads[5].wait()
    times(normed, wv, local_v, 512)

    first_q = [e for e in events if e[1] == 0 and e[2] == 0]
    rest_q = [e for e in events if e[1] or e[2]]
    middle = len(late) // 2
    for e in late[:middle]:
        arrived(0, e)

    @pl.loop(1, n)
    def _(k):
        spread(k).wait_recv()

    for d in range(n):
        t, c = d // 2, d % 2
        at = c * half_width + t // per_block * LANES
        down = t % per_block * piece
        write_q[down : down + piece, at : at + LANES] = pieces[d]
    attend_rows(
        write_q,
        mem_rows,
        local_k.at[pl.ds(tok_rows, mem_rows)],
        local_v.at[pl.ds(tok_rows, mem_rows)],
        tok_rows,
        all_rows,
        False,
    )
    tail = list(late[middle:])
    forwards = [e for e in tail if e[2] == 0]
    passed = tail.index(forwards[-1]) + 1 if forwards else 0
    for e in tail[:passed]:
        arrived(0, e)
    loads[2].wait()
    start(moves(1, 0, 0, 0))
    queue = list(first_q)
    for e in tail[passed:]:
        arrived(0, e)
        if queue:
            arrived(1, queue.pop(0))
    for e in queue:
        arrived(1, e)
    for e in everything:
        pair_arrive(0, *e)

    ahead = list(rest_q)

    def take(count):
        for _ in range(min(count, len(ahead))):
            arrived(1, ahead.pop(0))

    project(mem_rows)
    write_rows(0)
    send_kv(0)
    take(2)
    wait_kv(0)
    for step in range(1, ITERS):
        rk, rv = read_kv.at[step - 1, 0], read_kv.at[step - 1, 1]
        attend_rows(write_q, mem_rows, rk, rv, tok_rows, all_rows, False)
        project(mem_rows)
        write_rows(step)
        if step + 1 < ITERS:
            send_kv(step)
            take(2)
            wait_kv(step)
            take(2)
    store = pltpu.make_async_copy(previous, memory_out, store_sem.at[0])
    store.start()

    def share(k):
        to = lax.rem(me + k, n)
        return remote(change, changes.at[me], change_send.at[k], change_recv.at[k], to)

    @pl.loop(1, n)
    def _(k):
        share(k).start()

    changes[me] = change[...]

    plane_rows = block_rows[1] * 2 * side * side

    def query_plane(k):
        z = nearest(slow, k, depth)
        at = hint(z * plane_rows, LANES)
        tile = 512

        @pl.loop(0, query_width // tile)
        def _(t):
            cols = pl.ds(hint(t * tile, tile), tile)
            more = jnp.dot(
                normed[0:tok_rows, pl.ds(at, plane_rows)],
                wq[pl.ds(at, plane_rows), cols],
                preferred_element_type=f32,
            )
            if k == 0:
                query[:, cols] = more
            else:
                query[:, cols] += more

    for k in range(depth):
        while any(e[0] == k for e in ahead):
            take(1)
        for e in everything:
            if e[0] == k:
                pair_arrive(1, *e)
        query_plane(k)
    rk, rv = read_kv.at[ITERS - 2, 0], read_kv.at[ITERS - 2, 1]
    attend_rows(query, tok_rows, rk, rv, 0, tok_rows, True)
    project(tok_rows)

    @pl.loop(0, tok_rows // 16)
    def _(t):
        here = pl.ds(hint(t * 16, 16), 16)
        tokens[here, :] = layer_rows(tokens, here)

    store_tokens = pltpu.make_async_copy(tokens, token_out, store_sem.at[1])
    store_tokens.start()

    @pl.loop(1, n)
    def _(k):
        share(k).wait_recv()

    count_all = n * mem_rows * width
    total = changes[0]
    for d in range(1, n):
        total += changes[d]
    change_out[...] = jnp.sqrt(total / count_all + eps)

    swap.wait_send()
    for w in range(2):
        for e in everything:
            for guard, copy in moves(w, *e):
                if guard is None:
                    copy.wait_send()
                else:
                    pl.when(guard)(copy.wait_send)

    @pl.loop(1, chips)
    def _(k):
        scatter(k).wait_send()

    @pl.loop(1, n)
    def _(k):
        spread(k).wait_send()
        share(k).wait_send()

    @pl.when(me + 1 < n)
    def _():
        for step in range(ITERS - 1):
            for which in range(2):
                kv_copy(step, which).wait_send()

    store.wait()
    store_tokens.wait()


def fused(
    tokens,
    memory,
    norm_gain,
    post_gain,
    query_weight,
    key_matrix,
    value_matrix,
    output_weight,
    segment_weight,
):
    n = lax.axis_size("seg")
    chips = n // 2
    tok_rows, width = tokens.shape
    mem_rows = memory.shape[0]
    own_rows, query_width = query_weight.shape
    kv_width = key_matrix.shape[1]
    all_rows = tok_rows + mem_rows
    piece = mem_rows * (query_width // LANES) // n
    f32, bf16 = jnp.float32, jnp.bfloat16
    anywhere = pl.BlockSpec(memory_space=pl.ANY)
    in_vmem = pl.BlockSpec(memory_space=pltpu.VMEM)
    dma = pltpu.SemaphoreType.DMA
    outs = pl.pallas_call(
        functools.partial(fused_kernel, n),
        out_shape=(
            jax.ShapeDtypeStruct(tokens.shape, bf16),
            jax.ShapeDtypeStruct(memory.shape, bf16),
            jax.ShapeDtypeStruct((8, LANES), f32),
        ),
        in_specs=[
            anywhere,
            anywhere,
            in_vmem,
            in_vmem,
            anywhere,
            anywhere,
            anywhere,
            anywhere,
            pl.BlockSpec(memory_space=pltpu.SMEM),
        ],
        out_specs=(anywhere, anywhere, in_vmem),
        scratch_shapes=[
            pltpu.VMEM(tokens.shape, bf16),
            pltpu.VMEM(memory.shape, bf16),
            pltpu.VMEM(key_matrix.shape, bf16),
            pltpu.VMEM(value_matrix.shape, bf16),
            pltpu.VMEM((n * own_rows, query_width), bf16),
            pltpu.VMEM((query_width, width), bf16),
            pltpu.VMEM((256, query_width), bf16),
            pltpu.VMEM((all_rows, width), bf16),
            pltpu.VMEM((2, chips, piece, LANES), f32),
            pltpu.VMEM((chips, piece, LANES), f32),
            pltpu.VMEM((chips, piece, LANES), f32),
            pltpu.VMEM((chips, piece, LANES), f32),
            pltpu.VMEM((piece, LANES), bf16),
            pltpu.VMEM((n, piece, LANES), bf16),
            pltpu.VMEM((mem_rows, query_width), bf16),
            pltpu.VMEM((all_rows, kv_width), bf16),
            pltpu.VMEM((all_rows, kv_width), bf16),
            pltpu.VMEM((ITERS - 1, 2, mem_rows, kv_width), bf16),
            pltpu.VMEM((ITERS - 1, 2, mem_rows, kv_width), bf16),
            pltpu.VMEM((tok_rows, query_width), bf16),
            pltpu.VMEM((tok_rows, width), f32),
            pltpu.VMEM(memory.shape, bf16),
            pltpu.VMEM(memory.shape, bf16),
            pltpu.VMEM((tok_rows, query_width), f32),
            pltpu.VMEM((8, LANES), f32),
            pltpu.VMEM((n, 8, LANES), f32),
            dma((7,)),
            dma((2, chips * 5)),
            dma((2, chips)),
            dma((2, chips)),
            dma((2,)),
            dma((chips,)),
            dma((chips,)),
            dma((n,)),
            dma((n,)),
            dma((ITERS - 1, 2)),
            dma((ITERS - 1, 2)),
            dma((n,)),
            dma((n,)),
            dma((2,)),
        ],
        compiler_params=pltpu.CompilerParams(
            has_side_effects=True, vmem_limit_bytes=67_000_000
        ),
        name="segments",
    )(
        tokens,
        memory,
        norm_gain.reshape(1, width),
        post_gain.reshape(1, width),
        query_weight,
        key_matrix,
        value_matrix,
        output_weight,
        segment_weight,
    )
    return outs[0], outs[1], outs[2][0, :ITERS]


def solution(mesh):
    def step(*args):
        if fits(*args):
            return fused(*args)
        return shards(*args)

    in_specs = (
        P("seg", None),
        P(),
        P(),
        P(),
        P("seg", None),
        P(),
        P(),
        P("seg", None),
        P("seg"),
    )
    out_specs = (P("seg", None), P("seg", None), P())
    return jax.shard_map(
        step, mesh=mesh, in_specs=in_specs, out_specs=out_specs, check_vma=False
    )
```

profile of v0, /device:TPU:0, one launch (start us, length us, event | category | flops | bytes accessed | tf_op | source)
XLA Modules:
  0.0 170.2 jit_solution(5095632692424127751)
XLA Ops:
  1.3 1.3 reshape.12.norm_gain
  2.6 1.3 reshape.13.post_gain
  3.9 161.4 %segments.1 = (bf16[256,3584]{1,0:T(8,128)(2,1)}, bf16[64,3584]{1,0:T(8,128)(2,1)}, f32[8,128]{1,0:T(8,128)}) custom-call(bf16[256,3584]{1,0:T(8,128)(2,1)} %tokens_hbm.1, bf16[64,3584]{1,0:T(8,128)(2,1)} %memory_hbm.1, f32[1,3584]{1,0:T(1,128)} %reshape.12.norm_gain, f32[1,3584]{1,0:T(1,128)} %reshape.13.post_gain, bf16[112,2048]{1,0:T(8,128)(2,1)} %wq_hbm.1, ...), custom_call_target="tpu_custom_call" | custom-call | tf_op jit(solution)/shard_map/segments/pallas_call | solution.py:867
  165.4 1.2 slice_bitcast_fusion
  166.6 0.0 copy-start
  166.6 2.9 %copy.15 = bf16[256,3584]{1,0:T(8,128)(2,1)} copy(bf16[256,3584]{1,0:T(8,128)(2,1)} %get-tuple-element.12) | data formatting | bytes 3670016
  169.5 0.0 copy-done
  169.5 0.8 copy.16
Async XLA Ops:
  166.6 2.9 %copy-start = (bf16[64,3584]{1,0:T(8,128)(2,1)S(1)}, bf16[64,3584]{1,0:T(8,128)(2,1)}, u32[]{:S(2)}) copy-start(bf16[64,3584]{1,0:T(8,128)(2,1)} %get-tuple-element.13) | copy-start | bytes 1376260
where the time goes:
time: 173 us; the launch traced here: 170 us
  Pallas kernels  161 us (93%)
  local copies, waits for them, and re-layouts  7.52 us (4%)
    pallas_call x1, Pallas kernels, fused(): pl.pallas_call(functools.partial(fused_kernel, n), out_shape=(jax.ShapeDt...  161 us
    unnamed x4, local copies, waits for them, and re-layouts  3.67 us

commit v1 on v0

--- a/solution.py
+++ b/solution.py
@@ -297,6 +297,9 @@
         and own_rows % 16 == 0
         and out_rows % 16 == 0
         and (own_rows * plane) % LANES == 0
+        and (out_rows * plane) % LANES == 0
+        and own_rows > 16 * LAST_SLOW[1]
+        and out_rows > 16 * LAST_SLOW[0]
         and piece % 16 == 0
         and mem_rows % piece == 0
         and memory.shape[1] >= 256
@@ -312,19 +315,65 @@
     return value
 
 
-def arrival_order(depth, side):
-    sheet = sorted(
-        [(k, j) for k in range(depth) for j in range(side)],
-        key=lambda e: (e[0] + e[1], e[1] == 0, e[0]),
-    )
-    items, clock = [], 0
-    for k, j in sheet:
-        if k + j:
-            items.append((k + j, 0, (k, j, 0)))
-        clock = max(clock, k + j) + 1
-        for i in range(1, side):
-            items.append((clock + i - 1, 1, (k, j, i)))
-    return [e for _, _, e in sorted(items)]
+LAST_SLOW = (1, 1)
+DUE = (
+    (-11, 8, 13, 39, -2, 1),
+    (-5, 14, 16, 22, 15, 1),
+    (35, 13, 28, 71, -33, 1),
+    (59, 16, 7, 14, 24, 0),
+)
+STEPS = (
+    ("norm", -4),
+    ("swap", -4),
+    ("wk", 19),
+    ("wv", 22),
+    ("sum", 22),
+    ("attend1", 60),
+    ("p", (69, 69, 70, 70)),
+    ("kv1", 70),
+    ("a2", 85),
+    ("kv2", 85),
+    ("a3", 119),
+    ("f3", 119),
+    ("q", (136, 190, 222, 222)),
+    ("tail", 222),
+)
+
+
+def make_plan(depth, side, groups):
+    items = []
+    for g in groups:
+        base, by_k, by_j, by_i, both, lag = DUE[g]
+        for k in range(depth):
+            for j in range(side):
+                for i in range(side):
+                    due = base + by_k * k + by_j * j + by_i * i + both * j * i
+                    items.append((due, -2, g, (k, j, i)))
+                    if i == 0 and not (g % 2 and k):
+                        items.append((due + lag, -1, g, (k, j, i)))
+    last, count = -1000, 0
+    for name, at in STEPS:
+        for k in range(depth if isinstance(at, tuple) else 1):
+            due = at[min(k, len(at) - 1)] if isinstance(at, tuple) else at
+            last = max(last, due)
+            items.append((last, count, name, k))
+            count += 1
+    items.sort(key=lambda t: (t[0], max(t[1], -1), t[1]))
+    items = [(what, (which, order == -1)) if order < 0 else (what, which) for _, order, what, which in items]
+    blocks = [t for t in items if isinstance(t[0], int)]
+    plan = []
+
+    def add(op):
+        if op not in plan:
+            plan.append(op)
+
+    for what, which in items:
+        if what in ("p", "q"):
+            for g, e in blocks:
+                if g // 2 == (what == "q") and e[0][0] == which:
+                    add((g, e))
+        add((what, which))
+    return plan
 
 
 def fused_kernel(
@@ -367,6 +416,7 @@
     query,
     change,
     changes,
+    gains,
     load_sem,
     gather_send,
     gather_recv,
@@ -383,6 +433,13 @@
     store_sem,
 ):
     me = lax.axis_index("seg")
+    barrier = pltpu.get_barrier_semaphore()
+
+    @pl.loop(1, n)
+    def _(k):
+        to = lax.rem(me + k, n)
+        pl.semaphore_signal(barrier, inc=1, device_id=(to,), device_id_type=MESH)
+
     core = lax.rem(me, 2)
     partner = me + 1 - 2 * core
     chip = me // 2
@@ -414,6 +471,15 @@
         rows = block_rows[w]
         return full[w].at[pl.ds(hint(device * rows, 16), rows)]
 
+    cuts = [rows - 16 * LAST_SLOW[w] for w, rows in enumerate(block_rows)]
+    groups = [g for g in range(4) if g % 2 == 0 or LAST_SLOW[g // 2]]
+
+    def part_at(g, device):
+        w, rest = g // 2, g % 2
+        rows = 16 * LAST_SLOW[w] if rest else cuts[w]
+        begin = device * block_rows[w] + (cuts[w] if rest else 0)
+        return full[w].at[pl.ds(hint(begin, 16), rows)]
+
     def remote(src, dst, send, recv, device):
         return pltpu.make_async_remote_copy(
             src_ref=src,
@@ -433,22 +499,23 @@
     def rank(k, j, i):
         return (k * side + j) * side + i
 
-    def moves(w, k, j, i):
+    def moves(g, k, j, i):
         z, origin = place(k, j, i)
-        block = block_at(w, 2 * origin + core)
+        block = part_at(g, 2 * origin + core)
+        last = g % 2
         ports = 5
 
         def copy(port, device, recv):
             return remote(
                 block,
                 block,
-                gather_send.at[w, rank(k, j, i) * ports + port],
-                recv.at[w, origin],
+                gather_send.at[g, rank(k, j, i) * ports + port],
+                recv.at[g, origin],
                 device,
             )
 
         found = []
-        if j == 0 and i == 0:
+        if last or (j == 0 and i == 0):
             up = slow + 1 < depth
             down = slow > 0
             if k:
@@ -456,11 +523,11 @@
                 down = jnp.logical_and(down, z > slow)
             found.append((up, copy(0, me + 2 * z_step, gather_recv)))
             found.append((down, copy(1, me - 2 * z_step, gather_recv)))
-        if i == 0 and j == 0:
+        if j == 0 and i == 0 and not (last and k):
             found.append((None, copy(2, me + 2 * u_step * (1 - 2 * u), gather_recv)))
-        if i == 0:
+        found.append((None, copy(4, partner, pair_recv)))
+        if i == 0 and not (last and k):
             found.append((None, copy(3, me + 2 * v_step * (1 - 2 * v), gather_recv)))
-        found.append((None, copy(4, partner, pair_recv)))
         return found
 
     def start(items):
@@ -470,26 +537,38 @@
             else:
                 pl.when(guard)(copy.start)
 
-    def arrive(w, k, j, i):
+    def arrive(g, k, j, i):
         _, origin = place(k, j, i)
-        block = block_at(w, 2 * origin + core)
+        block = part_at(g, 2 * origin + core)
         remote(
-            block, block, gather_send.at[w, 0], gather_recv.at[w, origin], partner
+            block, block, gather_send.at[g, 0], gather_recv.at[g, origin], partner
         ).wait_recv()
 
-    def arrived(w, e):
-        arrive(w, *e)
-        start(moves(w, *e))
-
-    def pair_arrive(w, k, j, i):
-        _, origin = place(k, j, i)
-        block = block_at(w, 2 * origin + 1 - core)
-        remote(
-            block, block, gather_send.at[w, 0], pair_recv.at[w, origin], partner
-        ).wait_recv()
-
-    events = arrival_order(depth, side)
-    everything = [(0, 0, 0)] + events
+    def take(g, e, onward):
+        if onward:
+            start(moves(g, *e)[-1:])
+            return
+        if any(e):
+            arrive(g, *e)
+        first = moves(g, *e)
+        if e[2] == 0 and not (g % 2 and e[0]):
+            first = first[:-1]
+        start(first)
+
+    def pair_arrive(w, slow_rank):
+        for g in groups:
+            if g // 2 == w:
+                for j in range(side):
+                    for i in range(side):
+                        _, origin = place(slow_rank, j, i)
+                        block = part_at(g, 2 * origin + 1 - core)
+                        remote(
+                            block,
+                            block,
+                            gather_send.at[g, 0],
+                            pair_recv.at[g, origin],
+                            partner,
+                        ).wait_recv()
 
     def load(src, dst, i):
         return pltpu.make_async_copy(src, dst, load_sem.at[i])
@@ -513,6 +592,9 @@
     )
     own_window.start()
 
+    gains[0:1, :] = norm_gain[...].reshape(1, width)
+    gains[1:2, :] = post_gain[...].reshape(1, width)
+
     def norm_rows(src, dst, at, rows):
         step_rows = 16
 
@@ -522,7 +604,7 @@
             x = src[here, :].astype(f32)
             mean_sq = jnp.sum(x * x, axis=-1, keepdims=True) / width
             there = pl.ds(hint(at + t * step_rows, step_rows), step_rows)
-            dst[there, :] = (x / jnp.sqrt(mean_sq + eps) * norm_gain[...]).astype(bf16)
+            dst[there, :] = (x / jnp.sqrt(mean_sq + eps) * gains[0:1, :]).astype(bf16)
 
     def times(lhs, weight, dst, tile):
         @pl.loop(0, weight.shape[1] // tile)
@@ -572,11 +654,30 @@
                 attn[0:rows, :], wo[:, cols], preferred_element_type=f32
             )
 
+    out_rows = block_rows[0] * 2 * z_step
+
+    def project_plane(k):
+        at = hint(nearest(slow, k, depth) * out_rows, LANES)
+        tile = 512
+
+        @pl.loop(0, width // tile)
+        def _(t):
+            cols = pl.ds(hint(t * tile, tile), tile)
+            more = jnp.dot(
+                attn[0:mem_rows, pl.ds(at, out_rows)],
+                wo[pl.ds(at, out_rows), cols],
+                preferred_element_type=f32,
+            )
+            if k == 0:
+                proj[0:mem_rows, cols] = more
+            else:
+                proj[0:mem_rows, cols] += more
+
     def layer_rows(src, here):
         p = proj[here, :]
         mean_sq = jnp.sum(p * p, axis=-1, keepdims=True) / width
         x = src[here, :].astype(f32)
-        return (x + p / jnp.sqrt(mean_sq + eps) * post_gain[...]).astype(bf16)
+        return (x + p / jnp.sqrt(mean_sq + eps) * gains[1:2, :]).astype(bf16)
 
     def write_rows(step):
         before = memory if step == 0 else previous
@@ -594,7 +695,7 @@
             previous[here, :] = out
             if step + 1 < ITERS:
                 mean_sq = jnp.sum(o * o, axis=-1, keepdims=True) / width
-                newnorm[here, :] = (o / jnp.sqrt(mean_sq + eps) * norm_gain[...]).astype(bf16)
+                newnorm[here, :] = (o / jnp.sqrt(mean_sq + eps) * gains[0:1, :]).astype(bf16)
 
     right = lax.rem(me + 1, n)
 
@@ -623,31 +724,10 @@
             for which, local in enumerate((local_k, local_v)):
                 read_kv[step, which] = local[tok_rows:all_rows, :]
 
-    loads[0].wait()
-    start(moves(0, 0, 0, 0))
-    loads[1].wait()
-    norm_rows(memory, normed, tok_rows, mem_rows)
-    own_window.wait()
     piece = pieces.shape[1]
     per_block = mem_rows // piece
     half_width = query_width // 2
-    own_cols = normed[tok_rows:all_rows, pl.ds(hint(first_lane, LANES), 256)]
-    for c in range(2):
-        rows_of = jnp.dot(
-            own_cols,
-            window[:, c * half_width : (c + 1) * half_width],
-            preferred_element_type=f32,
-        )
-        for t in range(chips):
-            at = t // per_block * LANES
-            down = t % per_block * piece
-            part[c, t] = rows_of[down : down + piece, at : at + LANES]
     swap = remote(part.at[1 - core], swapped, swap_sem.at[0], swap_sem.at[1], partner)
-    swap.start()
-    loads[3].wait()
-    norm_rows(tokens, normed, 0, tok_rows)
-    swap.wait_recv()
-    kept[...] = part[core] + swapped[...]
 
     def scatter(k):
         to = lax.rem(chip + k, chips)
@@ -655,120 +735,129 @@
             kept.at[to], held.at[k], sum_send.at[k], sum_recv.at[k], 2 * to + core
         )
 
-    @pl.loop(1, chips)
-    def _(k):
-        scatter(k).start()
-
-    loads[4].wait()
-    times(normed, wk, local_k, 512)
-    early = [e for e in events if sum(e) == 1]
-    late = [e for e in events if sum(e) > 1]
-    for e in early:
-        arrived(0, e)
-
-    @pl.loop(1, chips)
-    def _(k):
-        scatter(k).wait_recv()
-
-    piece_sum = kept[chip]
-    for k in range(1, chips):
-        piece_sum += held[k]
-    piece_out[...] = (piece_sum * scale).astype(bf16)
-
     def spread(k):
         to = lax.rem(me + k, n)
         return remote(
             piece_out, pieces.at[me], spread_send.at[k], spread_recv.at[k], to
         )
 
-    @pl.loop(1, n)
-    def _(k):
-        spread(k).start()
-
-    pieces[me] = piece_out[...]
-    loads[5].wait()
-    times(normed, wv, local_v, 512)
-
-    first_q = [e for e in events if e[1] == 0 and e[2] == 0]
-    rest_q = [e for e in events if e[1] or e[2]]
-    middle = len(late) // 2
-    for e in late[:middle]:
-        arrived(0, e)
-
-    @pl.loop(1, n)
-    def _(k):
-        spread(k).wait_recv()
-
-    for d in range(n):
-        t, c = d // 2, d % 2
-        at = c * half_width + t // per_block * LANES
-        down = t % per_block * piece
-        write_q[down : down + piece, at : at + LANES] = pieces[d]
-    attend_rows(
-        write_q,
-        mem_rows,
-        local_k.at[pl.ds(tok_rows, mem_rows)],
-        local_v.at[pl.ds(tok_rows, mem_rows)],
-        tok_rows,
-        all_rows,
-        False,
-    )
-    tail = list(late[middle:])
-    forwards = [e for e in tail if e[2] == 0]
-    passed = tail.index(forwards[-1]) + 1 if forwards else 0
-    for e in tail[:passed]:
-        arrived(0, e)
-    loads[2].wait()
-    start(moves(1, 0, 0, 0))
-    queue = list(first_q)
-    for e in tail[passed:]:
-        arrived(0, e)
-        if queue:
-            arrived(1, queue.pop(0))
-    for e in queue:
-        arrived(1, e)
-    for e in everything:
-        pair_arrive(0, *e)
-
-    ahead = list(rest_q)
-
-    def take(count):
-        for _ in range(min(count, len(ahead))):
-            arrived(1, ahead.pop(0))
-
-    project(mem_rows)
-    write_rows(0)
-    send_kv(0)
-    take(2)
-    wait_kv(0)
-    for step in range(1, ITERS):
-        rk, rv = read_kv.at[step - 1, 0], read_kv.at[step - 1, 1]
-        attend_rows(write_q, mem_rows, rk, rv, tok_rows, all_rows, False)
-        project(mem_rows)
-        write_rows(step)
-        if step + 1 < ITERS:
-            send_kv(step)
-            take(2)
-            wait_kv(step)
-            take(2)
-    store = pltpu.make_async_copy(previous, memory_out, store_sem.at[0])
-    store.start()
-
     def share(k):
         to = lax.rem(me + k, n)
         return remote(change, changes.at[me], change_send.at[k], change_recv.at[k], to)
 
-    @pl.loop(1, n)
-    def _(k):
-        share(k).start()
-
-    changes[me] = change[...]
-
-    plane_rows = block_rows[1] * 2 * side * side
-
-    def query_plane(k):
-        z = nearest(slow, k, depth)
-        at = hint(z * plane_rows, LANES)
+    def step_norm(_):
+        loads[1].wait()
+        norm_rows(memory, normed, tok_rows, mem_rows)
+        own_window.wait()
+        own_cols = normed[tok_rows:all_rows, pl.ds(hint(first_lane, LANES), 256)]
+        for c in range(2):
+            rows_of = jnp.dot(
+                own_cols,
+                window[:, c * half_width : (c + 1) * half_width],
+                preferred_element_type=f32,
+            )
+            for t in range(chips):
+                at = t // per_block * LANES
+                down = t % per_block * piece
+                part[c, t] = rows_of[down : down + piece, at : at + LANES]
+        swap.start()
+
+    def step_swap(_):
+        loads[3].wait()
+        norm_rows(tokens, normed, 0, tok_rows)
+        swap.wait_recv()
+        kept[...] = part[core] + swapped[...]
+
+        @pl.loop(1, chips)
+        def _(k):
+            scatter(k).start()
+
+    def step_wk(_):
+        loads[4].wait()
+        times(normed, wk, local_k, 512)
+
+    def step_wv(_):
+        loads[5].wait()
+        times(normed, wv, local_v, 512)
+
+    def step_sum(_):
+        @pl.loop(1, chips)
+        def _(k):
+            scatter(k).wait_recv()
+
+        piece_sum = kept[chip]
+        for k in range(1, chips):
+            piece_sum += held[k]
+        piece_out[...] = (piece_sum * scale).astype(bf16)
+
+        @pl.loop(1, n)
+        def _(k):
+            spread(k).start()
+
+        pieces[me] = piece_out[...]
+
+    def step_attend1(_):
+        @pl.loop(1, n)
+        def _(k):
+            spread(k).wait_recv()
+
+        for d in range(n):
+            t, c = d // 2, d % 2
+            at = c * half_width + t // per_block * LANES
+            down = t % per_block * piece
+            write_q[down : down + piece, at : at + LANES] = pieces[d]
+        attend_rows(
+            write_q,
+            mem_rows,
+            local_k.at[pl.ds(tok_rows, mem_rows)],
+            local_v.at[pl.ds(tok_rows, mem_rows)],
+            tok_rows,
+            all_rows,
+            False,
+        )
+
+    def step_p(k):
+        pair_arrive(0, k)
+        project_plane(k)
+
+    def step_kv1(_):
+        write_rows(0)
+        send_kv(0)
+
+    def attend_write(step):
+        wait_kv(step)
+        rk, rv = read_kv.at[step, 0], read_kv.at[step, 1]
+        attend_rows(write_q, mem_rows, rk, rv, tok_rows, all_rows, False)
+
+    def step_a2(_):
+        attend_write(0)
+        project(mem_rows)
+        write_rows(1)
+
+    def step_kv2(_):
+        send_kv(1)
+
+    def step_a3(_):
+        attend_write(1)
+
+    store = pltpu.make_async_copy(previous, memory_out, store_sem.at[0])
+
+    def step_f3(_):
+        project(mem_rows)
+        write_rows(2)
+        store.start()
+
+        @pl.loop(1, n)
+        def _(k):
+            share(k).start()
+
+        changes[me] = change[...]
+
+    plane_rows = block_rows[1] * 2 * z_step
+
+    def step_q(k):
+        pair_arrive(1, k)
+        at = hint(nearest(slow, k, depth) * plane_rows, LANES)
         tile = 512
 
         @pl.loop(0, query_width // tile)
@@ -784,43 +873,69 @@
             else:
                 query[:, cols] += more
 
-    for k in range(depth):
-        while any(e[0] == k for e in ahead):
-            take(1)
-        for e in everything:
-            if e[0] == k:
-                pair_arrive(1, *e)
-        query_plane(k)
-    rk, rv = read_kv.at[ITERS - 2, 0], read_kv.at[ITERS - 2, 1]
-    attend_rows(query, tok_rows, rk, rv, 0, tok_rows, True)
-    project(tok_rows)
-
-    @pl.loop(0, tok_rows // 16)
-    def _(t):
-        here = pl.ds(hint(t * 16, 16), 16)
-        tokens[here, :] = layer_rows(tokens, here)
-
     store_tokens = pltpu.make_async_copy(tokens, token_out, store_sem.at[1])
-    store_tokens.start()
-
-    @pl.loop(1, n)
-    def _(k):
-        share(k).wait_recv()
-
-    count_all = n * mem_rows * width
-    total = changes[0]
-    for d in range(1, n):
-        total += changes[d]
-    change_out[...] = jnp.sqrt(total / count_all + eps)
+
+    def step_tail(_):
+        rk, rv = read_kv.at[ITERS - 2, 0], read_kv.at[ITERS - 2, 1]
+        attend_rows(query, tok_rows, rk, rv, 0, tok_rows, True)
+        project(tok_rows)
+
+        @pl.loop(0, tok_rows // 16)
+        def _(t):
+            here = pl.ds(hint(t * 16, 16), 16)
+            tokens[here, :] = layer_rows(tokens, here)
+
+        store_tokens.start()
+
+        @pl.loop(1, n)
+        def _(k):
+            share(k).wait_recv()
+
+        count_all = n * mem_rows * width
+        total = changes[0]
+        for d in range(1, n):
+            total += changes[d]
+        change_out[...] = jnp.sqrt(total / count_all + eps)
+
+    steps = {
+        "norm": step_norm,
+        "swap": step_swap,
+        "wk": step_wk,
+        "wv": step_wv,
+        "sum": step_sum,
+        "attend1": step_attend1,
+        "p": step_p,
+        "kv1": step_kv1,
+        "a2": step_a2,
+        "kv2": step_kv2,
+        "a3": step_a3,
+        "f3": step_f3,
+        "q": step_q,
+        "tail": step_tail,
+    }
+    plan = make_plan(depth, side, groups)
+    loads[0].wait()
+    pl.semaphore_wait(barrier, n - 1)
+    fetched = False
+    for what, which in plan:
+        if what in steps:
+            steps[what](which)
+        else:
+            if what // 2 and not fetched:
+                loads[2].wait()
+                fetched = True
+            take(what, *which)
 
     swap.wait_send()
-    for w in range(2):
-        for e in everything:
-            for guard, copy in moves(w, *e):
-                if guard is None:
-                    copy.wait_send()
-                else:
-                    pl.when(guard)(copy.wait_send)
+    for g, which in plan:
+        if g in steps or which[1]:
+            continue
+        e = which[0]
+        for guard, copy in moves(g, *e):
+            if guard is None:
+                copy.wait_send()
+            else:
+                pl.when(guard)(copy.wait_send)
 
     @pl.loop(1, chips)
     def _(k):
@@ -910,10 +1025,11 @@
             pltpu.VMEM((tok_rows, query_width), f32),
             pltpu.VMEM((8, LANES), f32),
             pltpu.VMEM((n, 8, LANES), f32),
+            pltpu.VMEM((2, width), f32),
             dma((7,)),
-            dma((2, chips * 5)),
-            dma((2, chips)),
-            dma((2, chips)),
+            dma((4, chips * 5)),
+            dma((4, chips)),
+            dma((4, chips)),
             dma((2,)),
             dma((chips,)),
             dma((chips,)),
@@ -926,14 +1042,14 @@
             dma((2,)),
         ],
         compiler_params=pltpu.CompilerParams(
-            has_side_effects=True, vmem_limit_bytes=67_000_000
+            collective_id=0, has_side_effects=True, vmem_limit_bytes=67_000_000
         ),
         name="segments",
     )(
         tokens,
         memory,
-        norm_gain.reshape(1, width),
-        post_gain.reshape(1, width),
+        norm_gain,
+        post_gain,
         query_weight,
         key_matrix,
         value_matrix,

time: 173 us -> 158 us (0.913); the launches traced: 170 us -> 158 us
  Pallas kernels: 161 us -> 152 us
  local copies, waits for them, and re-layouts: 7.52 us -> 4.86 us
    pallas_call x1, Pallas kernels: 161 us -> 152 us  [fused(): pl.pallas_call(functools.partial(fused_kernel, n), out_shape=(jax.ShapeDt...]
    reshape x2 -> x0, local copies, waits for them, and re-layouts: 2.65 us -> none  [the longest x1 1.33 us: fused(): norm_gain.reshape(1, width)]
where the time goes in v1:
time: 158 us
  Pallas kernels  152 us (96%)
  local copies, waits for them, and re-layouts  4.86 us (3%)
    pallas_call x1, Pallas kernels, fused(): pl.pallas_call(functools.partial(fused_kernel, n), out_shape=(jax.ShapeDt...  152 us
    unnamed x4, local copies, waits for them, and re-layouts  3.67 us

profile of v1, /device:TPU:0, one launch (start us, length us, event | category | flops | bytes accessed | tf_op | source)
XLA Modules:
  0.0 157.9 jit_solution(15979285495982855335)
XLA Ops:
  1.3 151.8 %segments.1 = (bf16[256,3584]{1,0:T(8,128)(2,1)}, bf16[64,3584]{1,0:T(8,128)(2,1)}, f32[8,128]{1,0:T(8,128)}) custom-call(bf16[256,3584]{1,0:T(8,128)(2,1)} %tokens_hbm.1, bf16[64,3584]{1,0:T(8,128)(2,1)} %memory_hbm.1, f32[3584]{0:T(1024)} %norm_gain.1, f32[3584]{0:T(1024)} %post_gain.1, bf16[112,2048]{1,0:T(8,128)(2,1)} %wq_hbm.1, ...), custom_call_target="tpu_custom_call" | custom-call | tf_op jit(solution)/shard_map/segments/pallas_call | solution.py:982
  153.0 1.2 slice_bitcast_fusion
  154.2 0.0 copy-start
  154.2 2.9 %copy.15 = bf16[256,3584]{1,0:T(8,128)(2,1)} copy(bf16[256,3584]{1,0:T(8,128)(2,1)} %get-tuple-element.12) | data formatting | bytes 3670016
  157.1 0.0 copy-done
  157.1 0.8 copy.16
Async XLA Ops:
  154.2 2.9 %copy-start = (bf16[64,3584]{1,0:T(8,128)(2,1)S(1)}, bf16[64,3584]{1,0:T(8,128)(2,1)}, u32[]{:S(2)}) copy-start(bf16[64,3584]{1,0:T(8,128)(2,1)} %get-tuple-element.13) | copy-start | bytes 1376260

commit v2 on v1

--- a/solution.py
+++ b/solution.py
@@ -301,6 +301,7 @@
         and own_rows > 16 * LAST_SLOW[1]
         and out_rows > 16 * LAST_SLOW[0]
         and piece % 16 == 0
+        and tokens.shape[0] % 64 == 0
         and mem_rows % piece == 0
         and memory.shape[1] >= 256
         and own_rows + LANES <= 256
@@ -315,6 +316,7 @@
     return value
 
 
+TILE = 896
 LAST_SLOW = (1, 1)
 DUE = (
     (-11, 8, 13, 39, -2, 1),
@@ -417,6 +419,7 @@
     change,
     changes,
     gains,
+    squares,
     load_sem,
     gather_send,
     gather_recv,
@@ -644,15 +647,29 @@
                 ) + jnp.dot(read.astype(bf16), rvv, preferred_element_type=f32)
                 attn[0:rows, cols] = (numer / denom).astype(bf16)
 
+    def add_squares(rows, p, first):
+        parts = p * p
+        total = parts[:, 0:LANES]
+        for c in range(LANES, p.shape[1], LANES):
+            total += parts[:, c : c + LANES]
+
+        @pl.when(first)
+        def _():
+            squares[0:rows, :] = total
+
+        @pl.when(jnp.logical_not(first))
+        def _():
+            squares[0:rows, :] += total
+
     def project(rows):
-        tile = 512
+        tile = TILE
 
         @pl.loop(0, width // tile)
         def _(t):
             cols = pl.ds(hint(t * tile, tile), tile)
-            proj[0:rows, cols] = jnp.dot(
-                attn[0:rows, :], wo[:, cols], preferred_element_type=f32
-            )
+            p = jnp.dot(attn[0:rows, :], wo[:, cols], preferred_element_type=f32)
+            proj[0:rows, cols] = p
+            add_squares(rows, p, t == 0)
 
     out_rows = block_rows[0] * 2 * z_step
 
@@ -671,18 +688,24 @@
             if k == 0:
                 proj[0:mem_rows, cols] = more
             else:
-                proj[0:mem_rows, cols] += more
+                more += proj[0:mem_rows, cols]
+                proj[0:mem_rows, cols] = more
+            if k == depth - 1:
+                add_squares(mem_rows, more, t == 0)
+
+    def divide_roots(rows):
+        mean_sq = jnp.sum(squares[0:rows, :], axis=-1, keepdims=True) / width
+        squares[0:rows, :] = jnp.broadcast_to(1.0 / jnp.sqrt(mean_sq + eps), (rows, LANES))
 
     def layer_rows(src, here):
-        p = proj[here, :]
-        mean_sq = jnp.sum(p * p, axis=-1, keepdims=True) / width
         x = src[here, :].astype(f32)
-        return (x + p / jnp.sqrt(mean_sq + eps) * gains[1:2, :]).astype(bf16)
+        return (x + proj[here, :] * squares[here, 0:1] * gains[1:2, :]).astype(bf16)
 
     def write_rows(step):
         before = memory if step == 0 else previous
         change[...] = jnp.zeros_like(change) if step == 0 else change[...]
         lane = lax.broadcasted_iota(jnp.int32, change.shape, 1)
+        divide_roots(mem_rows)
 
         @pl.loop(0, mem_rows // 16)
         def _(t):
@@ -724,7 +747,7 @@
             for which, local in enumerate((local_k, local_v)):
                 read_kv[step, which] = local[tok_rows:all_rows, :]
 
-    piece = pieces.shape[1]
+    piece = pieces.shape[2]
     per_block = mem_rows // piece
     half_width = query_width // 2
     swap = remote(part.at[1 - core], swapped, swap_sem.at[0], swap_sem.at[1], partner)
@@ -736,10 +759,18 @@
         )
 
     def spread(k):
-        to = lax.rem(me + k, n)
+        to = lax.rem(chip + k, chips)
         return remote(
-            piece_out, pieces.at[me], spread_send.at[k], spread_recv.at[k], to
+            piece_out,
+            pieces.at[core, chip],
+            spread_send.at[k],
+            spread_recv.at[k],
+            2 * to + core,
         )
+
+    hand_over = remote(
+        pieces.at[core], pieces.at[core], swap_sem.at[2], swap_sem.at[3], partner
+    )
 
     def share(k):
         to = lax.rem(me + k, n)
@@ -766,7 +797,9 @@
         loads[3].wait()
         norm_rows(tokens, normed, 0, tok_rows)
         swap.wait_recv()
-        kept[...] = part[core] + swapped[...]
+        both = part[core] + swapped[...]
+        kept[...] = both.astype(bf16)
+        swapped[...] = both
 
         @pl.loop(1, chips)
         def _(k):
@@ -785,27 +818,29 @@
         def _(k):
             scatter(k).wait_recv()
 
-        piece_sum = kept[chip]
+        piece_sum = swapped[chip]
         for k in range(1, chips):
-            piece_sum += held[k]
+            piece_sum += held[k].astype(f32)
         piece_out[...] = (piece_sum * scale).astype(bf16)
 
-        @pl.loop(1, n)
+        @pl.loop(1, chips)
         def _(k):
             spread(k).start()
 
-        pieces[me] = piece_out[...]
+        pieces[core, chip] = piece_out[...]
 
     def step_attend1(_):
-        @pl.loop(1, n)
+        @pl.loop(1, chips)
         def _(k):
             spread(k).wait_recv()
 
+        hand_over.start()
+        hand_over.wait()
         for d in range(n):
             t, c = d // 2, d % 2
             at = c * half_width + t // per_block * LANES
             down = t % per_block * piece
-            write_q[down : down + piece, at : at + LANES] = pieces[d]
+            write_q[down : down + piece, at : at + LANES] = pieces[c, t]
         attend_rows(
             write_q,
             mem_rows,
@@ -873,19 +908,28 @@
             else:
                 query[:, cols] += more
 
-    store_tokens = pltpu.make_async_copy(tokens, token_out, store_sem.at[1])
+    chunk = tok_rows // 4
+
+    def store_tokens(c):
+        rows = pl.ds(c * chunk, chunk)
+        return pltpu.make_async_copy(
+            tokens.at[rows], token_out.at[rows], store_sem.at[1 + c]
+        )
 
     def step_tail(_):
         rk, rv = read_kv.at[ITERS - 2, 0], read_kv.at[ITERS - 2, 1]
         attend_rows(query, tok_rows, rk, rv, 0, tok_rows, True)
         project(tok_rows)
-
-        @pl.loop(0, tok_rows // 16)
-        def _(t):
-            here = pl.ds(hint(t * 16, 16), 16)
-            tokens[here, :] = layer_rows(tokens, here)
-
-        store_tokens.start()
+        divide_roots(tok_rows)
+
+        for c in range(4):
+
+            @pl.loop(0, chunk // 16)
+            def _(t):
+                here = pl.ds(hint(c * chunk + t * 16, 16), 16)
+                tokens[here, :] = layer_rows(tokens, here)
+
+            store_tokens(c).start()
 
         @pl.loop(1, n)
         def _(k):
@@ -941,9 +985,10 @@
     def _(k):
         scatter(k).wait_send()
 
+        spread(k).wait_send()
+
     @pl.loop(1, n)
     def _(k):
-        spread(k).wait_send()
         share(k).wait_send()
 
     @pl.when(me + 1 < n)
@@ -953,7 +998,8 @@
                 kv_copy(step, which).wait_send()
 
     store.wait()
-    store_tokens.wait()
+    for c in range(4):
+        store_tokens(c).wait()
 
 
 def fused(
@@ -1009,10 +1055,10 @@
             pltpu.VMEM((all_rows, width), bf16),
             pltpu.VMEM((2, chips, piece, LANES), f32),
             pltpu.VMEM((chips, piece, LANES), f32),
-            pltpu.VMEM((chips, piece, LANES), f32),
-            pltpu.VMEM((chips, piece, LANES), f32),
+            pltpu.VMEM((chips, piece, LANES), bf16),
+            pltpu.VMEM((chips, piece, LANES), bf16),
             pltpu.VMEM((piece, LANES), bf16),
-            pltpu.VMEM((n, piece, LANES), bf16),
+            pltpu.VMEM((2, chips, piece, LANES), bf16),
             pltpu.VMEM((mem_rows, query_width), bf16),
             pltpu.VMEM((all_rows, kv_width), bf16),
             pltpu.VMEM((all_rows, kv_width), bf16),
@@ -1026,20 +1072,21 @@
             pltpu.VMEM((8, LANES), f32),
             pltpu.VMEM((n, 8, LANES), f32),
             pltpu.VMEM((2, width), f32),
+            pltpu.VMEM((tok_rows, LANES), f32),
             dma((7,)),
             dma((4, chips * 5)),
             dma((4, chips)),
             dma((4, chips)),
-            dma((2,)),
+            dma((4,)),
             dma((chips,)),
             dma((chips,)),
-            dma((n,)),
-            dma((n,)),
+            dma((chips,)),
+            dma((chips,)),
             dma((ITERS - 1, 2)),
             dma((ITERS - 1, 2)),
             dma((n,)),
             dma((n,)),
-            dma((2,)),
+            dma((5,)),
         ],
         compiler_params=pltpu.CompilerParams(
             collective_id=0, has_side_effects=True, vmem_limit_bytes=67_000_000

time: 158 us -> 155 us (0.981)
  Pallas kernels: 152 us -> 148 us
    pallas_call x1, Pallas kernels: 152 us -> 148 us  [fused(): pl.pallas_call(functools.partial(fused_kernel, n), out_shape=(jax.ShapeDt...]
where the time goes in v2:
time: 155 us; the launch traced here: 154 us
  Pallas kernels  148 us (95%)
  local copies, waits for them, and re-layouts  4.86 us (3%)
    pallas_call x1, Pallas kernels, fused(): pl.pallas_call(functools.partial(fused_kernel, n), out_shape=(jax.ShapeDt...  148 us
    unnamed x4, local copies, waits for them, and re-layouts  3.67 us

profile of v2, /device:TPU:0, one launch (start us, length us, event | category | flops | bytes accessed | tf_op | source)
XLA Modules:
  0.0 154.2 jit_solution(1797330881992340571)
XLA Ops:
  1.3 148.1 %segments.1 = (bf16[256,3584]{1,0:T(8,128)(2,1)}, bf16[64,3584]{1,0:T(8,128)(2,1)}, f32[8,128]{1,0:T(8,128)}) custom-call(bf16[256,3584]{1,0:T(8,128)(2,1)} %tokens_hbm.1, bf16[64,3584]{1,0:T(8,128)(2,1)} %memory_hbm.1, f32[3584]{0:T(1024)} %norm_gain.1, f32[3584]{0:T(1024)} %post_gain.1, bf16[112,2048]{1,0:T(8,128)(2,1)} %wq_hbm.1, ...), custom_call_target="tpu_custom_call" | custom-call | tf_op jit(solution)/shard_map/segments/pallas_call | solution.py:1028
  149.4 1.2 slice_bitcast_fusion
  150.5 0.0 copy-start
  150.6 2.9 %copy.15 = bf16[256,3584]{1,0:T(8,128)(2,1)} copy(bf16[256,3584]{1,0:T(8,128)(2,1)} %get-tuple-element.12) | data formatting | bytes 3670016
  153.5 0.0 copy-done
  153.5 0.8 copy.16
Async XLA Ops:
  150.5 2.9 %copy-start = (bf16[64,3584]{1,0:T(8,128)(2,1)S(1)}, bf16[64,3584]{1,0:T(8,128)(2,1)}, u32[]{:S(2)}) copy-start(bf16[64,3584]{1,0:T(8,128)(2,1)} %get-tuple-element.13) | copy-start | bytes 1376260

commit v3 on v2

--- a/solution.py
+++ b/solution.py
@@ -319,26 +319,26 @@
 TILE = 896
 LAST_SLOW = (1, 1)
 DUE = (
-    (-11, 8, 13, 39, -2, 1),
-    (-5, 14, 16, 22, 15, 1),
-    (35, 13, 28, 71, -33, 1),
-    (59, 16, 7, 14, 24, 0),
+    (-7, 9, 18, 77, 45, 1),
+    (-5, 11, 20, 26, 80, 1),
+    (24, 14, 38, 122, -24, 1),
+    (32, 19, 24, 43, -27, 0),
 )
 STEPS = (
-    ("norm", -4),
-    ("swap", -4),
-    ("wk", 19),
-    ("wv", 22),
-    ("sum", 22),
-    ("attend1", 60),
-    ("p", (69, 69, 70, 70)),
-    ("kv1", 70),
-    ("a2", 85),
-    ("kv2", 85),
-    ("a3", 119),
-    ("f3", 119),
-    ("q", (136, 190, 222, 222)),
-    ("tail", 222),
+    ("norm", -2),
+    ("swap", -2),
+    ("wk", -2),
+    ("wv", 18),
+    ("sum", 18),
+    ("attend1", 45),
+    ("p", (45, 61, 64, 64)),
+    ("kv1", 65),
+    ("a2", 87),
+    ("kv2", 89),
+    ("a3", 143),
+    ("f3", 169),
+    ("q", (192, 254, 284, 284)),
+    ("tail", 284),
 )
 
 

time: 155 us -> 152 us (0.981)
  Pallas kernels: 148 us -> 145 us
    pallas_call x1, Pallas kernels: 148 us -> 145 us  [fused(): pl.pallas_call(functools.partial(fused_kernel, n), out_shape=(jax.ShapeDt...]
where the time goes in v3:
time: 152 us
  Pallas kernels  145 us (95%)
  local copies, waits for them, and re-layouts  4.86 us (3%)
    pallas_call x1, Pallas kernels, fused(): pl.pallas_call(functools.partial(fused_kernel, n), out_shape=(jax.ShapeDt...  145 us
    unnamed x4, local copies, waits for them, and re-layouts  3.67 us

profile of v3, /device:TPU:0, one launch (start us, length us, event | category | flops | bytes accessed | tf_op | source)
XLA Modules:
  0.0 151.6 jit_solution(5623135115685291192)
XLA Ops:
  1.3 145.5 %segments.1 = (bf16[256,3584]{1,0:T(8,128)(2,1)}, bf16[64,3584]{1,0:T(8,128)(2,1)}, f32[8,128]{1,0:T(8,128)}) custom-call(bf16[256,3584]{1,0:T(8,128)(2,1)} %tokens_hbm.1, bf16[64,3584]{1,0:T(8,128)(2,1)} %memory_hbm.1, f32[3584]{0:T(1024)} %norm_gain.1, f32[3584]{0:T(1024)} %post_gain.1, bf16[112,2048]{1,0:T(8,128)(2,1)} %wq_hbm.1, ...), custom_call_target="tpu_custom_call" | custom-call | tf_op jit(solution)/shard_map/segments/pallas_call | solution.py:1028
  146.8 1.2 slice_bitcast_fusion
  148.0 0.0 copy-start
  148.0 2.9 %copy.15 = bf16[256,3584]{1,0:T(8,128)(2,1)} copy(bf16[256,3584]{1,0:T(8,128)(2,1)} %get-tuple-element.12) | data formatting | bytes 3670016
  150.9 0.0 copy-done
  150.9 0.8 copy.16
Async XLA Ops:
  148.0 2.9 %copy-start = (bf16[64,3584]{1,0:T(8,128)(2,1)S(1)}, bf16[64,3584]{1,0:T(8,128)(2,1)}, u32[]{:S(2)}) copy-start(bf16[64,3584]{1,0:T(8,128)(2,1)} %get-tuple-element.13) | copy-start | bytes 1376260
